TPU v7x, 32 devices: a whole 2x2x4 slice. The times are simulated.
32 devices in a mesh: dp: 16 (over z, x, core), tensor: 2 (over y).
Axes of the slice: x: 2, y: 2, z: 4, core: 2. Of those that a mesh axis runs over, the one named last changes fastest.
Arguments:
- x_in: bfloat16 [16, 2, 1024, 768], P(None, 'tensor', 'dp'), may hold values from -6 to 6
- cotangent: bfloat16 [16, 2, 1024, 768], P(None, 'tensor', 'dp'), may hold values from -6 to 6
- lengths: int32 [16], replicated, may hold values from 1 to 2048, 24576 in all
- dealing: int32 [16], replicated, may hold values from 0 to 15, each once
- w_qkv: float32 [768, 3, 768], P('dp', None, 'tensor'), may hold values from -0.21875 to 0.21875
- w_out: float32 [768, 768], P('dp', 'tensor'), may hold values from -1.75 to 1.75
- w_in: float32 [768, 3072], P('dp', 'tensor'), may hold values from -0.21875 to 0.21875
- w_ffo: float32 [768, 3072], P('dp', 'tensor'), may hold values from -0.109375 to 0.109375
- b_qv: float32 [2, 768], P(None, 'tensor'), may hold values from -3 to 3
- b_out: float32 [768], replicated, may hold values from -3 to 3
- b_in: float32 [3072], P('tensor'), may hold values from -3 to 3
- b_ffo: float32 [768], replicated, may hold values from -3 to 3
- ln1_gain: float32 [768], replicated, may hold values from 0.1 to 1.9
- ln1_bias: float32 [768], replicated, may hold values from -3 to 3
- ln2_gain: float32 [768], replicated, may hold values from 0.1 to 1.9
- ln2_bias: float32 [768], replicated, may hold values from -3 to 3
Outputs:
- out: bfloat16 [16, 2, 1024, 768], P(None, 'tensor', 'dp')
- grad_in: bfloat16 [16, 2, 1024, 768], P(None, 'tensor', 'dp')
- grad_w_qkv: float32 [768, 3, 768], P('dp', None, 'tensor')
- grad_w_out: float32 [768, 768], P('dp', 'tensor')
- grad_w_in: float32 [768, 3072], P('dp', 'tensor')
- grad_w_ffo: float32 [768, 3072], P('dp', 'tensor')
- grad_b_qv: float32 [2, 768], P(None, 'tensor')
- grad_b_out: float32 [768], replicated
- grad_b_in: float32 [3072], P('tensor')
- grad_b_ffo: float32 [768], replicated
- grad_ln1_gain: float32 [768], replicated
- grad_ln1_bias: float32 [768], replicated
- grad_ln2_gain: float32 [768], replicated
- grad_ln2_bias: float32 [768], replicated
Inputs may be any that keep to these rules, and one draw needn't show every extreme that they name: Slot j holds lengths[j] tokens of its sequence and padding after them; some slot is full, 2048 tokens. Sequence s goes to slot dealing[s]; every slot gets one sequence.
All inputs are finite; a program needn't handle non-finite values.
Results may differ from a plain program's by a relative error of at most 0.018.
Values may be sent and summed in bfloat16 or wider, within the bound.
A program may use at most 192 MiB of HBM per device.

v0:
```python
import jax
import jax.numpy as jnp
from jax import lax
from jax.sharding import PartitionSpec as P

HEAD_DIM = 64


def slot_owner(dealing):
    places = jnp.arange(dealing.shape[0], dtype=jnp.int32)
    matches = dealing[None, :] == places[:, None]
    return jnp.sum(jnp.where(matches, places[None, :], 0), axis=1)


def contract_last(left_side, right_side):
    return lax.dot_general(
        left_side, right_side, (((1,), (1,)), ((), ())), preferred_element_type=jnp.float32
    )


def contract_first(left_side, right_side):
    return lax.dot_general(
        left_side, right_side, (((0,), (0,)), ((), ())), preferred_element_type=jnp.float32
    )


def norm_forward(values, norm_gain, norm_shift):
    centre = jnp.mean(values, axis=-1, keepdims=True)
    centred = values - centre
    inverse = lax.rsqrt(jnp.mean(centred * centred, axis=-1, keepdims=True) + 1e-06)
    normed = centred * inverse
    return (normed * norm_gain + norm_shift, normed, inverse)


def norm_backward(upstream, normed, inverse, norm_gain):
    scaled = upstream * norm_gain
    back_rows = inverse * (
        scaled
        - jnp.mean(scaled, axis=-1, keepdims=True)
        - normed * jnp.mean(scaled * normed, axis=-1, keepdims=True)
    )
    return (back_rows, jnp.sum(upstream * normed, axis=0), jnp.sum(upstream, axis=0))


def gelu_slope(values):
    return (
        0.5 * (1.0 + lax.erf(values * 0.7071067811865476))
        + values * jnp.exp(-0.5 * values * values) * 0.3989422804014327
    )


def head_forward(query_rows, key_rows, value_rows, key_valid, block_rows, score_scale):
    outputs = []
    totals = []
    for row_start in range(0, query_rows.shape[0], block_rows):
        scores = (
            contract_last(query_rows[row_start : row_start + block_rows], key_rows) * score_scale
        )
        scores = jnp.where(key_valid[None, :], scores, -jnp.inf)
        maxima = jnp.max(scores, axis=1, keepdims=True)
        weights = jnp.exp(scores - maxima)
        summed = jnp.sum(weights, axis=1, keepdims=True)
        probs_low = (weights / summed).astype(jnp.bfloat16)
        outputs.append(jnp.dot(probs_low, value_rows, preferred_element_type=jnp.float32))
        totals.append((maxima + jnp.log(summed))[:, 0])
    return (jnp.concatenate(outputs, axis=0), jnp.concatenate(totals, axis=0))


def head_backward(
    query_rows, key_rows, value_rows, mixed_grad, log_totals, key_valid, block_rows, score_scale
):
    key_grad = jnp.zeros(key_rows.shape, jnp.float32)
    value_grad = jnp.zeros(value_rows.shape, jnp.float32)
    query_parts = []
    for row_start in range(0, query_rows.shape[0], block_rows):
        query_block = query_rows[row_start : row_start + block_rows]
        grad_block = mixed_grad[row_start : row_start + block_rows]
        scores = contract_last(query_block, key_rows) * score_scale
        scores = jnp.where(key_valid[None, :], scores, -jnp.inf)
        probs = jnp.exp(scores - log_totals[row_start : row_start + block_rows][:, None])
        prob_grad = contract_last(grad_block, value_rows)
        shared = jnp.sum(probs * prob_grad, axis=1, keepdims=True)
        score_grad = (probs * (prob_grad - shared)).astype(jnp.bfloat16)
        query_parts.append(
            jnp.dot(score_grad, key_rows, preferred_element_type=jnp.float32) * score_scale
        )
        key_grad = key_grad + contract_first(score_grad, query_block) * score_scale
        value_grad = value_grad + contract_first(probs.astype(jnp.bfloat16), grad_block)
    return (jnp.concatenate(query_parts, axis=0), key_grad, value_grad)


def per_device(
    x_in,
    cotangent,
    lengths,
    dealing,
    w_qkv,
    w_out,
    w_in,
    w_ffo,
    b_qv,
    b_out,
    b_in,
    b_ffo,
    ln1_gain,
    ln1_bias,
    ln2_gain,
    ln2_bias,
):
    owners = slot_owner(dealing)
    dealt_x, dealt_grad = (
        lax.all_to_all(
            jnp.take(x_in, owners, axis=0), "dp", split_axis=0, concat_axis=2, tiled=True
        ),
        lax.all_to_all(
            jnp.take(cotangent, owners, axis=0), "dp", split_axis=0, concat_axis=2, tiled=True
        ),
    )
    tokens_half = dealt_x[0, 0]
    output_grad = dealt_grad[0, 0].astype(jnp.float32)
    half_rows = tokens_half.shape[0]
    tensor_count = lax.axis_size("tensor")
    tensor_index = lax.axis_index("tensor")
    seq_rows = half_rows * tensor_count
    model_width = tokens_half.shape[1]
    head_width = b_qv.shape[1]
    head_count = head_width // HEAD_DIM
    ffn_width = b_in.shape[0]
    block_rows = min(512, seq_rows)
    score_scale = HEAD_DIM ** (-0.5)
    key_valid = jnp.arange(seq_rows) < lengths[lax.axis_index("dp")]
    qkv_weight, out_weight, in_weight, ffo_weight = (
        lax.all_gather(w_qkv.astype(jnp.bfloat16), "dp", axis=0, tiled=True),
        lax.all_gather(w_out.astype(jnp.bfloat16), "dp", axis=0, tiled=True),
        lax.all_gather(w_in.astype(jnp.bfloat16), "dp", axis=0, tiled=True),
        lax.all_gather(w_ffo.astype(jnp.bfloat16), "dp", axis=0, tiled=True),
    )

    def split_heads(matrix):
        return matrix.reshape(seq_rows, head_count, HEAD_DIM).transpose(1, 0, 2)

    def merge_heads(stacked):
        return stacked.transpose(1, 0, 2).reshape(seq_rows, head_width)

    tokens_full = lax.all_gather(tokens_half, "tensor", axis=0, tiled=True)
    projected = jnp.einsum(
        "ld,dce->cle", tokens_full, qkv_weight, preferred_element_type=jnp.float32
    )
    query_heads = split_heads((projected[0] + b_qv[0]).astype(jnp.bfloat16))
    key_heads = split_heads(projected[1].astype(jnp.bfloat16))
    value_heads = split_heads((projected[2] + b_qv[1]).astype(jnp.bfloat16))
    mixed_heads, log_totals = lax.map(
        lambda triple: head_forward(
            triple[0], triple[1], triple[2], key_valid, block_rows, score_scale
        ),
        (query_heads, key_heads, value_heads),
    )
    mixed_low = merge_heads(mixed_heads).astype(jnp.bfloat16)
    attn_half = lax.psum_scatter(
        contract_last(
            lax.slice_in_dim(mixed_low, 0, lax.axis_size("tensor") * half_rows, axis=0), out_weight
        ).astype(jnp.bfloat16),
        "tensor",
        scatter_dimension=0,
        tiled=True,
    ).astype(jnp.float32)
    first_norm, normed_one, inverse_one = norm_forward(
        tokens_half.astype(jnp.float32) + attn_half + b_out, ln1_gain, ln1_bias
    )
    first_full = lax.all_gather(first_norm.astype(jnp.bfloat16), "tensor", axis=0, tiled=True)
    hidden = jnp.dot(first_full, in_weight, preferred_element_type=jnp.float32) + b_in
    active = jax.nn.gelu(hidden, approximate=False).astype(jnp.bfloat16)
    ffn_half = lax.psum_scatter(
        contract_last(
            lax.slice_in_dim(active, 0, lax.axis_size("tensor") * half_rows, axis=0), ffo_weight
        ).astype(jnp.bfloat16),
        "tensor",
        scatter_dimension=0,
        tiled=True,
    ).astype(jnp.float32)
    result, normed_two, inverse_two = norm_forward(
        first_norm + ffn_half + b_ffo, ln2_gain, ln2_bias
    )
    final_grad, gain_two_grad, shift_two_grad = norm_backward(
        output_grad, normed_two, inverse_two, ln2_gain
    )
    ffo_bias_grad = jnp.sum(final_grad, axis=0)
    qkv_weight, out_weight, in_weight, ffo_weight = (
        lax.all_gather(w_qkv.astype(jnp.bfloat16), "dp", axis=0, tiled=True),
        lax.all_gather(w_out.astype(jnp.bfloat16), "dp", axis=0, tiled=True),
        lax.all_gather(w_in.astype(jnp.bfloat16), "dp", axis=0, tiled=True),
        lax.all_gather(w_ffo.astype(jnp.bfloat16), "dp", axis=0, tiled=True),
    )
    ffn_grad_full = lax.all_gather(final_grad.astype(jnp.bfloat16), "tensor", axis=0, tiled=True)
    ffo_weight_grad = contract_first(ffn_grad_full, active)
    hidden_grad = (
        jnp.dot(ffn_grad_full, ffo_weight, preferred_element_type=jnp.float32) * gelu_slope(hidden)
    ).astype(jnp.bfloat16)
    in_weight_grad = contract_first(first_full, hidden_grad)
    in_bias_grad = jnp.sum(hidden_grad.astype(jnp.float32), axis=0)
    first_grad = final_grad + lax.psum_scatter(
        contract_last(
            lax.slice_in_dim(hidden_grad, 0, lax.axis_size("tensor") * half_rows, axis=0), in_weight
        ).astype(jnp.bfloat16),
        "tensor",
        scatter_dimension=0,
        tiled=True,
    ).astype(jnp.float32)
    resid_grad, gain_one_grad, shift_one_grad = norm_backward(
        first_grad, normed_one, inverse_one, ln1_gain
    )
    out_bias_grad = jnp.sum(resid_grad, axis=0)
    attn_grad_full = lax.all_gather(resid_grad.astype(jnp.bfloat16), "tensor", axis=0, tiled=True)
    out_weight_grad = contract_first(attn_grad_full, mixed_low)
    mixed_grad = jnp.dot(attn_grad_full, out_weight, preferred_element_type=jnp.float32).astype(
        jnp.bfloat16
    )
    query_grads, key_grads, value_grads = lax.map(
        lambda bundle: head_backward(
            bundle[0],
            bundle[1],
            bundle[2],
            bundle[3],
            bundle[4],
            key_valid,
            block_rows,
            score_scale,
        ),
        (query_heads, key_heads, value_heads, split_heads(mixed_grad), log_totals),
    )
    qkv_grad = jnp.stack(
        [merge_heads(query_grads), merge_heads(key_grads), merge_heads(value_grads)]
    ).astype(jnp.bfloat16)
    qv_bias_grad = jnp.stack(
        [
            jnp.sum(qkv_grad[0].astype(jnp.float32), axis=0),
            jnp.sum(qkv_grad[2].astype(jnp.float32), axis=0),
        ]
    )
    qkv_weight_grad = jnp.einsum(
        "ld,cle->dce", tokens_full, qkv_grad, preferred_element_type=jnp.float32
    )
    rows_grad = lax.slice_in_dim(qkv_grad, 0, lax.axis_size("tensor") * half_rows, axis=1)
    input_grad = resid_grad + lax.psum_scatter(
        jnp.einsum("cle,dce->ld", rows_grad, qkv_weight, preferred_element_type=jnp.float32).astype(
            jnp.bfloat16
        ),
        "tensor",
        scatter_dimension=0,
        tiled=True,
    ).astype(jnp.float32)
    qkv_sum, out_sum, in_sum, ffo_sum = (
        lax.psum_scatter(qkv_weight_grad, "dp", scatter_dimension=0, tiled=True),
        lax.psum_scatter(out_weight_grad, "dp", scatter_dimension=0, tiled=True),
        lax.psum_scatter(in_weight_grad, "dp", scatter_dimension=0, tiled=True),
        lax.psum_scatter(ffo_weight_grad, "dp", scatter_dimension=0, tiled=True),
    )
    norm_terms = jnp.stack(
        [out_bias_grad, ffo_bias_grad, gain_one_grad, shift_one_grad, gain_two_grad, shift_two_grad]
    )
    qv_padded = lax.dynamic_update_slice_in_dim(
        jnp.zeros((2, model_width), jnp.float32), qv_bias_grad, tensor_index * head_width, 1
    )
    in_padded = lax.dynamic_update_slice_in_dim(
        jnp.zeros((ffn_width * tensor_count,), jnp.float32),
        in_bias_grad,
        tensor_index * ffn_width,
        0,
    )
    norm_sums, qv_sums, in_sums = lax.psum((norm_terms, qv_padded, in_padded), ("dp", "tensor"))
    qv_share = lax.dynamic_slice_in_dim(qv_sums, tensor_index * head_width, head_width, 1)
    in_share = lax.dynamic_slice_in_dim(in_sums, tensor_index * ffn_width, ffn_width, 0)
    back_out, back_grad = (
        lax.all_to_all(
            result.astype(jnp.bfloat16)[None, None], "dp", split_axis=2, concat_axis=0, tiled=True
        ),
        lax.all_to_all(
            input_grad.astype(jnp.bfloat16)[None, None],
            "dp",
            split_axis=2,
            concat_axis=0,
            tiled=True,
        ),
    )
    return (
        jnp.take(back_out, dealing, axis=0),
        jnp.take(back_grad, dealing, axis=0),
        qkv_sum,
        out_sum,
        in_sum,
        ffo_sum,
        qv_share,
        norm_sums[0],
        in_share,
        norm_sums[1],
        norm_sums[2],
        norm_sums[3],
        norm_sums[4],
        norm_sums[5],
    )


def solution(mesh):
    return jax.shard_map(
        per_device,
        mesh=mesh,
        in_specs=(
            P(None, "tensor", "dp", None),
            P(None, "tensor", "dp", None),
            P(),
            P(),
            P("dp", None, "tensor"),
            P("dp", "tensor"),
            P("dp", "tensor"),
            P("dp", "tensor"),
            P(None, "tensor"),
            P(),
            P("tensor"),
            P(),
            P(),
            P(),
            P(),
            P(),
        ),
        out_specs=(
            P(None, "tensor", "dp", None),
            P(None, "tensor", "dp", None),
            P("dp", None, "tensor"),
            P("dp", "tensor"),
            P("dp", "tensor"),
            P("dp", "tensor"),
            P(None, "tensor"),
            P(),
            P("tensor"),
            P(),
            P(),
            P(),
            P(),
            P(),
        ),
        check_vma=False,
    )
```

profile of v0, /device:TPU:0, one launch (start us, length us, event | category | flops | bytes accessed | tf_op | source)
XLA Modules:
  0.0 1286.9 jit_solution(3330152919851395239)
XLA Ops:
  16.4 53.0 %all_to_all.42 = bf16[16,1,64,768]{3,2,1,0:T(8,128)(2,1)} all-to-all(bf16[16,1,64,768]{3,2,1,0:T(8,128)(2,1)S(1)} %get-tuple-element.272), channel_id=1, replica_groups=mesh['dp'=16,'tensor'=2] {'dp'}, dimensions={0} | all-to-all | bytes 3145728 | tf_op jit(solution)/shard_map/all_to_all | solution.py:112
  70.2 23.6 %all_gather.30 = bf16[768,384]{1,0:T(8,128)(2,1)} all-gather(bf16[48,384]{1,0:T(8,128)(2,1)S(1)} %convert_element_type.160), channel_id=1, replica_groups=mesh['dp'=16,'tensor'=2] {'dp'}, dimensions={0}, use_global_device_ids=true | all-gather | bytes 626688 | tf_op jit(solution)/shard_map/all_gather | solution.py:134
  93.8 20.8 %all-gather.8.cloned.1.call-done = bf16[2048,768]{1,0:T(8,128)(2,1)} async-done(((bf16[1024,768]{1,0:T(8,128)(2,1)}), bf16[2048,768]{1,0:T(8,128)(2,1)}) %all-gather.8.cloned.1.call-update) | async-done | bytes 3145744 | tf_op jit(solution)/shard_map/all_gather | solution.py:145
  114.7 6.5 convolution_bitcast_fusion
  122.5 3.0 fusion.154
  125.6 3.1 copy.69
  128.6 5.8 copy.68
  134.4 5.7 copy.70
  140.1 5.2 fusion.129
  148.9 117.0 %while.28 = (s32[]{:T(128)}, bf16[6,2048,64]{1,2,0:T(8,128)(2,1)}, f32[6,2048]{1,0:T(8,128)}, bf16[6,2048,64]{2,1,0:T(8,128)(2,1)}, bf16[6,2048,64]{2,1,0:T(8,12...) while((s32[]{:T(128)}, bf16[6,2048,64]{1,2,0:T(8,128)(2,1)}, ...), condition=%wide.region_10.12_spmd.clone, body=%wide.region_1.11_spmd.clone.sunk | while | flops 1125128192 | bytes 70637272 | solution.py:152
  155.0 3.5 fusion.240
  159.8 2.9 fusion.241
  174.4 3.5 fusion.240
  179.2 2.9 fusion.241
  193.8 3.5 fusion.240
  198.6 2.9 fusion.241
  213.2 3.5 fusion.240
  218.0 2.9 fusion.241
  232.6 3.5 fusion.240
  237.4 2.9 fusion.241
  252.0 3.5 fusion.240
  256.8 2.9 fusion.241
  265.9 6.2 convolution_convert_fusion
  273.8 41.9 %reduce-scatter.9.cloned.1.call-done = bf16[1024,768]{1,0:T(8,128)(2,1)} async-done(((bf16[2048,768]{1,0:T(8,128)(2,1)}), bf16[1024,768]{1,0:T(8,128)(2,1)}) %reduce-scatter.9.cloned.1.call-update) | async-done | bytes 1572880 | tf_op jit(solution)/shard_map/reduce_scatter | solution.py:159
  321.6 39.1 %all-gather.14.cloned.1.call-done = bf16[768,1536]{1,0:T(8,128)(2,1)} async-done(((bf16[48,1536]{1,0:T(8,128)(2,1)}), bf16[768,1536]{1,0:T(8,128)(2,1)}) %all-gather.14.cloned.1.call-update) | async-done | bytes 2359312 | tf_op jit(solution)/shard_map/all_gather | solution.py:135
  360.7 45.1 %all-gather.12.cloned.1.call-done = bf16[2048,768]{1,0:T(8,128)(2,1)} async-done(((bf16[1024,768]{1,0:T(8,128)(2,1)}), bf16[2048,768]{1,0:T(8,128)(2,1)}) %all-gather.12.cloned.1.call-update) | async-done | bytes 3145744 | tf_op jit(solution)/shard_map/all_gather | solution.py:170
  405.8 34.6 %fusion.115 = (bf16[2048,1536]{1,0:T(8,128)(2,1)}, f32[2048,1536]{1,0:T(8,128)}) fusion(f32[1536]{0:T(1024)S(1)} %copy-done.49, bf16[2048,768]{1,0:T(8,128)(2,1)} %all-gather.12.cloned.1.call-done, bf16[768,1536]{1,0:T(8,128)(2,1)} %all-gather.14.cloned.1.call-done), kind=kOutput, calls=%fused_computation.175 | convolution fusion | flops 5039456256 | bytes 24385536 | tf_op jit(solution)/shard_map/dot_general | solution.py:171
  440.4 10.5 all-gather.16.cloned.1.call-done
  450.8 9.0 convolution_convert_fusion.2
  460.0 40.0 %all_to_all.43 = bf16[16,1,64,768]{3,2,1,0:T(8,128)(2,1)S(1)} all-to-all(bf16[16,1,64,768]{3,2,1,0:T(8,128)(2,1)} %get-tuple-element.271), channel_id=1, replica_groups=mesh['dp'=16,'tensor'=2] {'dp'}, dimensions={0} | all-to-all | bytes 3145728 | tf_op jit(solution)/shard_map/all_to_all | solution.py:115
  502.5 2.9 fusion.153
  508.6 3.4 fusion.151
  512.0 45.3 %all-gather.18.cloned.1.call-done = bf16[2048,768]{1,0:T(8,128)(2,1)} async-done(((bf16[1024,768]{1,0:T(8,128)(2,1)}), bf16[2048,768]{1,0:T(8,128)(2,1)}) %all-gather.18.cloned.1.call-update) | async-done | bytes 3145744 | tf_op jit(solution)/shard_map/all_gather | solution.py:194
  557.3 12.4 convert_reduce_fusion
  572.3 6.4 convolution_convert_fusion.1
  578.8 43.5 %reduce-scatter.13.cloned.1.call-done = bf16[1024,768]{1,0:T(8,128)(2,1)} async-done(((bf16[2048,768]{1,0:T(8,128)(2,1)}), bf16[1024,768]{1,0:T(8,128)(2,1)}) %reduce-scatter.13.cloned.1.call-update) | async-done | bytes 1572880 | tf_op jit(solution)/shard_map/reduce_scatter | solution.py:201
  622.4 4.6 multiply_reduce_fusion.4
  632.4 45.0 %all-gather.20.cloned.1.call-done = bf16[2048,768]{1,0:T(8,128)(2,1)} async-done(((bf16[1024,768]{1,0:T(8,128)(2,1)}), bf16[2048,768]{1,0:T(8,128)(2,1)}) %all-gather.20.cloned.1.call-update) | async-done | bytes 3145744 | tf_op jit(solution)/shard_map/all_gather | solution.py:213
  677.4 3.3 convolution_convert_fusion.3
  680.8 2.9 copy.72
  687.6 217.3 %while.29 = (s32[]{:T(128)}, bf16[6,2048,64]{1,2,0:T(8,128)(2,1)}, bf16[6,2048,64]{1,2,0:T(8,128)(2,1)}, bf16[6,2048,64]{1,2,0:T(8,128)(2,1)}, bf16[6,2048,64]{2...) while((s32[]{:T(128)}, bf16[6,2048,64]{1,2,0:T(8,128)(2,1)}, ...), condition=%wide.region_27.29_spmd.clone, body=%wide.region_22.28_spmd.clone.sunk | while | flops 2724331520 | bytes 161284432 | solution.py:218
  910.9 8.5 bitcast_convert_fusion
  921.3 9.6 fusion.157
  932.8 9.5 fusion.156
  943.7 4.8 fusion.155
  948.5 3.8 copy.87
  952.8 11.5 reduce.24
  964.3 4.7 reshape.275
  969.0 5.7 all-to-all-start.1
  974.7 8.7 fusion.138
  989.8 11.5 reduce.23
  1001.3 4.6 reshape.277
  1005.9 9.2 all-to-all-done.1
  1015.1 19.2 %all-to-all-start.3 = ((bf16[16,2,24576]{2,1,0:T(2,128)(2,1)}), bf16[16,2,24576]{2,1,0:T(2,128)(2,1)}, u32[]{:S(2)}, u32[]{:S(2)}) async-start(bf16[16,2,24576]{2,1,0:T(2,128)(2,1)} %reshape.277), calls=%async_computation.7 | async-start | bytes 3145728 | tf_op jit(solution)/shard_map/all_to_all | solution.py:277
  1034.4 10.1 reshape.276
  1044.5 3.4 copy.82
  1047.9 3.3 gather_fusion.1
  1052.3 48.6 %all-reduce = (f32[2,768]{1,0:T(2,128)S(1)}, f32[6,768]{1,0:T(8,128)S(1)}, f32[3072]{0:T(1024)S(1)}) all-reduce(f32[2,768]{1,0:T(2,128)S(1)} %maximum_dynamic-update-slice_fusion, f32[6,768]{1,0:T(8,128)S(1)} %stack.44, f32[3072]{0:T(1024)S(1)} %dynamic_update_slice.24), channel_id=1, replica_groups=mesh['dp'=16,'tensor'=2] {'dp','tensor'}, use_global_device_ids=true, to_apply=%region_35.37 | all-reduce | flops 9216 | bytes 73728 | tf_op jit(solution)/shard_map/psum | solution.py:270
  1102.8 8.1 reshape.278
  1112.3 3.3 gather_fusion.3
  1115.7 3.5 fusion.145
  1119.2 28.1 %reduce-scatter.21.cloned.1.call-done = f32[48,1536]{1,0:T(8,128)} async-done(((f32[768,1536]{1,0:T(8,128)}), f32[48,1536]{1,0:T(8,128)}) %reduce-scatter.21.cloned.1.call-update) | async-done | bytes 294928 | tf_op jit(solution)/shard_map/reduce_scatter | solution.py:255
  1147.3 61.5 %reduce-scatter.19.cloned.1.call-done = f32[48,384]{1,0:T(8,128)} async-done(((f32[768,384]{1,0:T(8,128)}), f32[48,384]{1,0:T(8,128)}) %reduce-scatter.19.cloned.1.call-update) | async-done | bytes 73744 | tf_op jit(solution)/shard_map/reduce_scatter | solution.py:254
  1208.7 71.4 %reduce-scatter.17.cloned.1.call-done = f32[48,3,384]{2,0,1:T(8,128)} async-done(((f32[768,3,384]{2,0,1:T(8,128)}), f32[48,3,384]{2,0,1:T(8,128)}) %reduce-scatter.17.cloned.1.call-update) | async-done | bytes 221200 | tf_op jit(solution)/shard_map/reduce_scatter | solution.py:253
  (484 shorter events, 356.2 us)
Async XLA Ops:
  7.2 5.0 copy-start
  7.2 86.6 %all-gather.10.cloned.1.call-start = ((), (), s32[]{:S(2)}) async-start(), calls=%async_computation.13 | async-start | bytes 1880064 | tf_op jit(solution)/shard_map/all_gather | solution.py:133
  9.0 105.7 %all-gather.8.cloned.1.call-start = ((), (), s32[]{:S(2)}) async-start(), calls=%async_computation.12 | async-start | bytes 4718592 | tf_op jit(solution)/shard_map/all_gather | solution.py:145
  16.4 53.1 %copy-start.43 = (f32[2,384]{1,0:T(2,128)S(1)}, f32[2,384]{1,0:T(2,128)}, u32[]{:S(2)}) copy-start(f32[2,384]{1,0:T(2,128)} %param.30) | copy-start | bytes 9220
  16.4 53.3 %copy-start.30 = (f32[48,384]{1,0:T(8,128)S(1)}, f32[48,384]{1,0:T(8,128)}, u32[]{:S(2)}) copy-start(f32[48,384]{1,0:T(8,128)} %param.27) | copy-start | bytes 221188
  16.4 53.3 %copy-start.50 = (s32[16]{0:T(128)S(1)}, s32[16]{0:T(128)}, u32[]{:S(2)}) copy-start(s32[16]{0:T(128)} %param.24) | copy-start | bytes 196
  69.4 246.3 %reduce-scatter.9.cloned.1.call-start = ((), (), s32[]{:S(2)}) async-start(), calls=%async_computation.14 | async-start | bytes 4718592 | tf_op jit(solution)/shard_map/reduce_scatter | solution.py:159
  140.1 5.2 copy-start.11
  155.0 3.5 copy-start.5
  174.4 3.5 copy-start.5
  193.8 3.5 copy-start.5
  213.2 3.5 copy-start.5
  232.6 3.5 copy-start.5
  252.0 3.5 copy-start.5
  265.9 6.2 copy-start.2
  272.0 43.6 %copy-start.29 = (f32[768]{0:T(1024)S(1)}, f32[768]{0:T(1024)}, u32[]{:S(2)}) copy-start(f32[768]{0:T(1024)} %param.31) | copy-start | bytes 9220
  272.0 43.6 %copy-start.4 = (bf16[16,1,64,768]{3,2,1,0:T(8,128)(2,1)S(1)}, bf16[16,1,64,768]{3,2,1,0:T(8,128)(2,1)}, u32[]{:S(2)}) copy-start(bf16[16,1,64,768]{3,2,1,0:T(8,128)(2,1)} %all_to_all.42) | copy-start | bytes 4718596
  272.1 88.6 %all-gather.14.cloned.1.call-start = ((), (), s32[]{:S(2)}) async-start(), calls=%async_computation.16 | async-start | bytes 2506752 | tf_op jit(solution)/shard_map/all_gather | solution.py:135
  273.7 45.0 %copy-start.31 = (f32[768]{0:T(1024)S(1)}, f32[768]{0:T(1024)}, u32[]{:S(2)}) copy-start(f32[768]{0:T(1024)} %param.34) | copy-start | bytes 9220
  273.7 45.0 %copy-start.38 = (f32[768]{0:T(1024)S(1)}, f32[768]{0:T(1024)}, u32[]{:S(2)}) copy-start(f32[768]{0:T(1024)} %param.35) | copy-start | bytes 9220
  273.7 132.0 %all-gather.12.cloned.1.call-start = ((), (), s32[]{:S(2)}) async-start(), calls=%async_computation.15 | async-start | bytes 4718592 | tf_op jit(solution)/shard_map/all_gather | solution.py:170
  318.7 87.1 %copy-start.49 = (f32[1536]{0:T(1024)S(1)}, f32[1536]{0:T(1024)}, u32[]{:S(2)}) copy-start(f32[1536]{0:T(1024)} %param.32) | copy-start | bytes 18436
  320.8 130.0 %all-gather.16.cloned.1.call-start = ((), (), s32[]{:S(2)}) async-start(), calls=%async_computation.17 | async-start | bytes 2506752 | tf_op jit(solution)/shard_map/all_gather | solution.py:136
  321.6 180.9 %reduce-scatter.11.cloned.1.call-start = ((), (), s32[]{:S(2)}) async-start(), calls=%async_computation.18 | async-start | bytes 4718592 | tf_op jit(solution)/shard_map/reduce_scatter | solution.py:173
  459.9 41.2 %copy-start.32 = (f32[768]{0:T(1024)S(1)}, f32[768]{0:T(1024)}, u32[]{:S(2)}) copy-start(f32[768]{0:T(1024)} %param.36) | copy-start | bytes 9220
  459.9 42.6 %copy-start.41 = (f32[768]{0:T(1024)S(1)}, f32[768]{0:T(1024)}, u32[]{:S(2)}) copy-start(f32[768]{0:T(1024)} %param.33) | copy-start | bytes 9220
  459.9 97.4 %all-gather.18.cloned.1.call-start = ((), (), s32[]{:S(2)}) async-start(), calls=%async_computation.19 | async-start | bytes 4718592 | tf_op jit(solution)/shard_map/all_gather | solution.py:194
  512.0 110.4 %reduce-scatter.13.cloned.1.call-start = ((), (), s32[]{:S(2)}) async-start(), calls=%async_computation.20 | async-start | bytes 4718592 | tf_op jit(solution)/shard_map/reduce_scatter | solution.py:201
  557.3 15.1 %copy-start.48 = (bf16[768,1536]{1,0:T(8,128)(2,1)S(1)}, bf16[768,1536]{1,0:T(8,128)(2,1)}, u32[]{:S(2)}) copy-start(bf16[768,1536]{1,0:T(8,128)(2,1)} %all-gather.14.cloned.1.call-done) | copy-start | bytes 7077892
  578.8 98.7 %all-gather.20.cloned.1.call-start = ((), (), s32[]{:S(2)}) async-start(), calls=%async_computation.21 | async-start | bytes 4718592 | tf_op jit(solution)/shard_map/all_gather | solution.py:213
  622.4 4.6 copy-start.10
  622.4 4.6 copy-start.21
  631.1 46.4 %copy-start.26 = (bf16[768,384]{1,0:T(8,128)(2,1)S(1)}, bf16[768,384]{1,0:T(8,128)(2,1)}, u32[]{:S(2)}) copy-start(bf16[768,384]{1,0:T(8,128)(2,1)} %all_gather.30) | copy-start | bytes 1769476
  632.4 351.1 %reduce-scatter.15.cloned.1.call-start = ((), (), s32[]{:S(2)}) async-start(), calls=%async_computation.22 | async-start | bytes 4718592 | tf_op jit(solution)/shard_map/reduce_scatter | solution.py:244
  683.6 4.0 copy-start.3
  687.8 3.6 copy-start.6
  724.0 3.6 copy-start.6
  760.1 3.6 copy-start.6
  796.2 3.6 copy-start.6
  832.4 3.6 copy-start.6
  868.5 3.6 copy-start.6
  904.9 2.8 copy-start.16
  904.9 4.4 copy-start.14
  919.5 199.7 %reduce-scatter.23.cloned.1.call-start = ((), (), s32[]{:S(2)}) async-start(), calls=%async_computation.26 | async-start | bytes 5013504 | tf_op jit(solution)/shard_map/reduce_scatter | solution.py:256
  930.9 216.3 %reduce-scatter.21.cloned.1.call-start = ((), (), s32[]{:S(2)}) async-start(), calls=%async_computation.25 | async-start | bytes 5013504 | tf_op jit(solution)/shard_map/reduce_scatter | solution.py:255
  942.3 266.4 %reduce-scatter.19.cloned.1.call-start = ((), (), s32[]{:S(2)}) async-start(), calls=%async_computation.24 | async-start | bytes 1253376 | tf_op jit(solution)/shard_map/reduce_scatter | solution.py:254
  964.3 10.4 copy-start.23
  964.3 10.4 copy-start.24
  969.0 46.1 %all-to-all-start.1 = ((bf16[16,2,24576]{2,1,0:T(2,128)(2,1)}), bf16[16,2,24576]{2,1,0:T(2,128)(2,1)}, u32[]{:S(2)}, u32[]{:S(2)}) async-start(bf16[16,2,24576]{2,1,0:T(2,128)(2,1)} %reshape.275), calls=%async_computation.3 | async-start | bytes 3145728 | tf_op jit(solution)/shard_map/all_to_all | solution.py:274
  974.7 305.5 %reduce-scatter.17.cloned.1.call-start = ((), (), s32[]{:S(2)}) async-start(), calls=%async_computation.23 | async-start | bytes 3760128 | tf_op jit(solution)/shard_map/reduce_scatter | solution.py:253
  1001.3 33.0 %copy-start.45 = (s32[16]{0:T(128)S(1)}, s32[16]{0:T(128)}, u32[]{:S(2)}) copy-start(s32[16]{0:T(128)} %get-tuple-element.277) | copy-start | bytes 196
  1001.3 33.0 %copy-start.36 = (f32[768]{0:T(1024)S(1)}, f32[768]{0:T(1024)}, u32[]{:S(2)}) copy-start(f32[768]{0:T(1024)} %get-tuple-element.194) | copy-start | bytes 9220
  1001.3 33.1 %copy-start.39 = (f32[768]{0:T(1024)S(1)}, f32[768]{0:T(1024)}, u32[]{:S(2)}) copy-start(f32[768]{0:T(1024)} %get-tuple-element.189) | copy-start | bytes 9220
  1015.1 87.7 %all-to-all-start.3 = ((bf16[16,2,24576]{2,1,0:T(2,128)(2,1)}), bf16[16,2,24576]{2,1,0:T(2,128)(2,1)}, u32[]{:S(2)}, u32[]{:S(2)}) async-start(bf16[16,2,24576]{2,1,0:T(2,128)(2,1)} %reshape.277), calls=%async_computation.7 | async-start | bytes 3145728 | tf_op jit(solution)/shard_map/all_to_all | solution.py:277
  1044.5 6.8 copy-start.40
  1044.5 7.1 copy-start.35
  1044.5 7.1 copy-start.34
  1044.5 7.1 copy-start.33
  1044.5 7.1 copy-start.37
  1044.5 7.2 copy-start.17
  1047.9 4.0 copy-start.15
  1110.9 4.7 copy-start.44
  1112.3 3.3 copy-start.20
  1115.7 164.5 %copy-start.1 = (bf16[16,1,64,768]{3,2,1,0:T(8,128)(2,1)S(1)}, bf16[16,1,64,768]{3,2,1,0:T(8,128)(2,1)}, u32[]{:S(2)}) copy-start(bf16[16,1,64,768]{3,2,1,0:T(8,128)(2,1)} %param.23) | copy-start | bytes 4718596
  (25 other events, 44.9 us)
Sparse Core Ops, SparseCore 0:
  10.9 53.5 all-gather.9
  69.5 45.1 all-gather.7
  272.2 43.4 reduce-scatter.8
  318.4 42.2 all-gather.13
  362.1 43.6 all-gather.11
  408.5 42.2 all-gather.15
  460.0 42.1 reduce-scatter.10
  512.1 45.1 all-gather.17
  578.9 43.4 reduce-scatter.12
  632.5 44.8 all-gather.19
  919.6 43.4 reduce-scatter.14
  967.3 94.5 reduce-scatter.22
  1066.4 80.8 reduce-scatter.20
  1151.3 57.3 reduce-scatter.18
  1213.0 67.1 reduce-scatter.16
where the time goes:
time: 1300 us; the launch traced here: 1290 us
  waiting for transfers between devices  462 us (36%)
  matrix products  388 us (30%)
  blocking collectives  165 us (13%)
  local copies, waits for them, and re-layouts  116 us (9%)
  other arithmetic  113 us (9%)
  starting transfers between devices  25.9 us (2%)
  between operations  14.7 us (1%)
    dot_general x75, matrix products, contract_last(): lax.dot_general(left_side, right_side, (((1,), (1,)), ((), ())), preferre...  168 us
    dot_general x51, matrix products, contract_first(): lax.dot_general(left_side, right_side, (((0,), (0,)), ((), ())), preferre...  97.7 us
    reduce_scatter x1, waiting for transfers between devices, per_device(): lax.psum_scatter(qkv_weight_grad, 'dp', scatter_dimension=0, tiled=True)  71.4 us
    reduce_scatter x1, waiting for transfers between devices, per_device(): lax.psum_scatter(out_weight_grad, 'dp', scatter_dimension=0, tiled=True)  61.5 us
    all_to_all x1, blocking collectives, per_device(): lax.all_to_all(jnp.take(x_in, owners, axis=0), 'dp', split_axis=0, concat...  53 us
    psum x1, blocking collectives, per_device(): lax.psum((norm_terms, qv_padded, in_padded), ('dp', 'tensor'))  48.6 us
    unnamed x103, local copies, waits for them, and re-layouts  46.6 us
    all_gather x1, waiting for transfers between devices, per_device(): lax.all_gather(final_grad.astype(jnp.bfloat16), 'tensor', axis=0, tiled=T...  45.3 us
  transfers between devices with their start and end apart: 17, of which 12 were waited for; matrix products, arithmetic and copies ran while one was open for 12% of the time, Pallas kernels for 0%

commit v1 on v0

--- a/solution.py
+++ b/solution.py
@@ -4,6 +4,18 @@
 from jax.sharding import PartitionSpec as P
 
 HEAD_DIM = 64
+
+
+def doubled_up(x, axis, dim):
+    ways, here, hop = (lax.axis_size(axis), lax.axis_index(axis), x.shape[dim])
+    line, have = (x, 1)
+    while have < ways:
+        line = jnp.concatenate(
+            [line, lax.ppermute(line, axis, [(d, (d - have) % ways) for d in range(ways)])],
+            axis=dim,
+        )
+        have = 2 * have
+    return jnp.roll(line, here * hop, axis=dim)
 
 
 def slot_owner(dealing):
@@ -167,7 +179,7 @@
     first_norm, normed_one, inverse_one = norm_forward(
         tokens_half.astype(jnp.float32) + attn_half + b_out, ln1_gain, ln1_bias
     )
-    first_full = lax.all_gather(first_norm.astype(jnp.bfloat16), "tensor", axis=0, tiled=True)
+    first_full = doubled_up(first_norm.astype(jnp.bfloat16), "tensor", 0)
     hidden = jnp.dot(first_full, in_weight, preferred_element_type=jnp.float32) + b_in
     active = jax.nn.gelu(hidden, approximate=False).astype(jnp.bfloat16)
     ffn_half = lax.psum_scatter(

time: 1300 us -> 1250 us (0.962)
  waiting for transfers between devices: 462 us -> 408 us
    all_gather x1 -> x0, waiting for transfers between devices: 45.1 us -> none  [per_device(): lax.all_gather(first_norm.astype(jnp.bfloat16), 'tensor', axis=0, tiled=T...]
    all_gather x1, waiting for transfers between devices: 39.1 us -> 0.01 us  [per_device(): lax.all_gather(w_in.astype(jnp.bfloat16), 'dp', axis=0, tiled=True)]
    ppermute x0 -> x1, waiting for transfers between devices: none -> 35.1 us  [doubled_up(): lax.ppermute(line, axis, [(d, (d - have) % ways) for d in range(ways)])]
  transfers between devices with their start and end apart: 17 -> 17, of which waited for: 12 -> 11; matrix products, arithmetic and copies ran while one was open for 12% -> 13% of each run, Pallas kernels for 0% -> 0%
where the time goes in v1:
time: 1250 us; the launch traced here: 1240 us
  waiting for transfers between devices  408 us (33%)
  matrix products  388 us (31%)
  blocking collectives  165 us (13%)
  other arithmetic  119 us (10%)
  local copies, waits for them, and re-layouts  116 us (9%)
  starting transfers between devices  26.2 us (2%)
  between operations  14.7 us (1%)
    dot_general x75, matrix products, contract_last(): lax.dot_general(left_side, right_side, (((1,), (1,)), ((), ())), preferre...  168 us
    dot_general x51, matrix products, contract_first(): lax.dot_general(left_side, right_side, (((0,), (0,)), ((), ())), preferre...  97.7 us
    reduce_scatter x1, waiting for transfers between devices, per_device(): lax.psum_scatter(qkv_weight_grad, 'dp', scatter_dimension=0, tiled=True)  71.6 us
    reduce_scatter x1, waiting for transfers between devices, per_device(): lax.psum_scatter(out_weight_grad, 'dp', scatter_dimension=0, tiled=True)  61.6 us
    all_to_all x1, blocking collectives, per_device(): lax.all_to_all(jnp.take(x_in, owners, axis=0), 'dp', split_axis=0, concat...  53 us
    psum x1, blocking collectives, per_device(): lax.psum((norm_terms, qv_padded, in_padded), ('dp', 'tensor'))  48.7 us
    unnamed x103, local copies, waits for them, and re-layouts  46.6 us
    all_gather x1, waiting for transfers between devices, per_device(): lax.all_gather(final_grad.astype(jnp.bfloat16), 'tensor', axis=0, tiled=T...  45.3 us
  transfers between devices with their start and end apart: 17, of which 11 were waited for; matrix products, arithmetic and copies ran while one was open for 13% of the time, Pallas kernels for 0%

profile of v1, /device:TPU:0, one launch (start us, length us, event | category | flops | bytes accessed | tf_op | source)
XLA Modules:
  0.0 1240.5 jit_solution(11277169149185792513)
XLA Ops:
  16.4 53.0 %all_to_all.42 = bf16[16,1,64,768]{3,2,1,0:T(8,128)(2,1)} all-to-all(bf16[16,1,64,768]{3,2,1,0:T(8,128)(2,1)S(1)} %get-tuple-element.272), channel_id=1, replica_groups=mesh['dp'=16,'tensor'=2] {'dp'}, dimensions={0} | all-to-all | bytes 3145728 | tf_op jit(solution)/shard_map/all_to_all | solution.py:124
  70.2 23.6 %all_gather.27 = bf16[768,384]{1,0:T(8,128)(2,1)} all-gather(bf16[48,384]{1,0:T(8,128)(2,1)S(1)} %convert_element_type.160), channel_id=1, replica_groups=mesh['dp'=16,'tensor'=2] {'dp'}, dimensions={0}, use_global_device_ids=true | all-gather | bytes 626688 | tf_op jit(solution)/shard_map/all_gather | solution.py:146
  93.8 20.8 %all-gather.7.cloned.1.call-done = bf16[2048,768]{1,0:T(8,128)(2,1)} async-done(((bf16[1024,768]{1,0:T(8,128)(2,1)}), bf16[2048,768]{1,0:T(8,128)(2,1)}) %all-gather.7.cloned.1.call-update) | async-done | bytes 3145744 | tf_op jit(solution)/shard_map/all_gather | solution.py:157
  114.7 6.5 convolution_bitcast_fusion
  122.5 3.0 fusion.157
  125.6 3.1 copy.69
  128.6 5.8 copy.68
  134.4 5.7 copy.70
  140.1 5.2 fusion.129
  148.9 117.0 %while.28 = (s32[]{:T(128)}, bf16[6,2048,64]{1,2,0:T(8,128)(2,1)}, f32[6,2048]{1,0:T(8,128)}, bf16[6,2048,64]{2,1,0:T(8,128)(2,1)}, bf16[6,2048,64]{2,1,0:T(8,12...) while((s32[]{:T(128)}, bf16[6,2048,64]{1,2,0:T(8,128)(2,1)}, ...), condition=%wide.region_10.12_spmd.clone, body=%wide.region_1.11_spmd.clone.sunk | while | flops 1125128192 | bytes 70637272 | solution.py:164
  155.0 3.5 fusion.243
  159.8 2.9 fusion.244
  174.4 3.5 fusion.243
  179.2 2.9 fusion.244
  193.8 3.5 fusion.243
  198.6 2.9 fusion.244
  213.2 3.5 fusion.243
  218.0 2.9 fusion.244
  232.6 3.5 fusion.243
  237.4 2.9 fusion.244
  252.0 3.5 fusion.243
  256.8 2.9 fusion.244
  265.9 6.2 convolution_convert_fusion
  273.8 41.9 %reduce-scatter.9.cloned.1.call-done = bf16[1024,768]{1,0:T(8,128)(2,1)} async-done(((bf16[2048,768]{1,0:T(8,128)(2,1)}), bf16[1024,768]{1,0:T(8,128)(2,1)}) %reduce-scatter.9.cloned.1.call-update) | async-done | bytes 1572880 | tf_op jit(solution)/shard_map/reduce_scatter | solution.py:171
  321.9 35.1 %collective-permute-done = bf16[1024,768]{1,0:T(8,128)(2,1)} collective-permute-done((bf16[1024,768]{1,0:T(8,128)(2,1)}, bf16[1024,768]{1,0:T(8,128)(2,1)}, u32[]{:S(2)}, u32[]{:S(2)}) %collective-permute-start) | collective-permute-done | bytes 1572896 | tf_op jit(solution)/shard_map/ppermute | solution.py:14
  357.0 6.6 fusion.133
  363.6 34.6 %fusion.115 = (bf16[2048,1536]{1,0:T(8,128)(2,1)}, f32[2048,1536]{1,0:T(8,128)}) fusion(f32[1536]{0:T(1024)S(1)} %copy-done.49, bf16[2048,768]{1,0:T(8,128)(2,1)} %fusion.133, bf16[768,1536]{1,0:T(8,128)(2,1)} %all-gather.11.cloned.1.call-done), kind=kOutput, calls=%fused_computation.175 | convolution fusion | flops 5039456256 | bytes 24385536 | tf_op jit(solution)/shard_map/dot_general | solution.py:183
  398.2 6.1 all-gather.13.cloned.1.call-done
  404.3 9.0 convolution_convert_fusion.2
  413.4 40.0 %all_to_all.43 = bf16[16,1,64,768]{3,2,1,0:T(8,128)(2,1)S(1)} all-to-all(bf16[16,1,64,768]{3,2,1,0:T(8,128)(2,1)} %get-tuple-element.271), channel_id=1, replica_groups=mesh['dp'=16,'tensor'=2] {'dp'}, dimensions={0} | all-to-all | bytes 3145728 | tf_op jit(solution)/shard_map/all_to_all | solution.py:127
  456.0 2.9 fusion.156
  462.1 3.4 fusion.154
  465.5 45.3 %all-gather.15.cloned.1.call-done = bf16[2048,768]{1,0:T(8,128)(2,1)} async-done(((bf16[1024,768]{1,0:T(8,128)(2,1)}), bf16[2048,768]{1,0:T(8,128)(2,1)}) %all-gather.15.cloned.1.call-update) | async-done | bytes 3145744 | tf_op jit(solution)/shard_map/all_gather | solution.py:206
  510.8 12.4 convert_reduce_fusion
  525.8 6.4 convolution_convert_fusion.1
  532.3 43.5 %reduce-scatter.13.cloned.1.call-done = bf16[1024,768]{1,0:T(8,128)(2,1)} async-done(((bf16[2048,768]{1,0:T(8,128)(2,1)}), bf16[1024,768]{1,0:T(8,128)(2,1)}) %reduce-scatter.13.cloned.1.call-update) | async-done | bytes 1572880 | tf_op jit(solution)/shard_map/reduce_scatter | solution.py:213
  575.9 4.6 multiply_reduce_fusion.4
  585.9 45.0 %all-gather.17.cloned.1.call-done = bf16[2048,768]{1,0:T(8,128)(2,1)} async-done(((bf16[1024,768]{1,0:T(8,128)(2,1)}), bf16[2048,768]{1,0:T(8,128)(2,1)}) %all-gather.17.cloned.1.call-update) | async-done | bytes 3145744 | tf_op jit(solution)/shard_map/all_gather | solution.py:225
  630.9 3.3 convolution_convert_fusion.3
  634.3 2.9 copy.72
  641.1 217.3 %while.29 = (s32[]{:T(128)}, bf16[6,2048,64]{1,2,0:T(8,128)(2,1)}, bf16[6,2048,64]{1,2,0:T(8,128)(2,1)}, bf16[6,2048,64]{1,2,0:T(8,128)(2,1)}, bf16[6,2048,64]{2...) while((s32[]{:T(128)}, bf16[6,2048,64]{1,2,0:T(8,128)(2,1)}, ...), condition=%wide.region_27.29_spmd.clone, body=%wide.region_22.28_spmd.clone.sunk | while | flops 2724331520 | bytes 161284432 | solution.py:230
  864.4 8.5 bitcast_convert_fusion
  874.8 9.6 fusion.160
  886.3 9.5 fusion.159
  897.2 4.8 fusion.158
  902.0 3.8 copy.87
  906.3 11.5 reduce.24
  917.8 4.7 reshape.275
  922.5 5.6 all-to-all-start.1
  928.2 8.7 fusion.141
  943.2 11.5 reduce.23
  954.8 4.6 reshape.277
  959.4 9.2 all-to-all-done.1
  968.6 19.2 %all-to-all-start.3 = ((bf16[16,2,24576]{2,1,0:T(2,128)(2,1)}), bf16[16,2,24576]{2,1,0:T(2,128)(2,1)}, u32[]{:S(2)}, u32[]{:S(2)}) async-start(bf16[16,2,24576]{2,1,0:T(2,128)(2,1)} %reshape.277), calls=%async_computation.7 | async-start | bytes 3145728 | tf_op jit(solution)/shard_map/all_to_all | solution.py:289
  987.9 10.1 reshape.276
  998.0 3.4 copy.82
  1001.4 3.3 gather_fusion.1
  1005.7 48.7 %all-reduce = (f32[2,768]{1,0:T(2,128)S(1)}, f32[6,768]{1,0:T(8,128)S(1)}, f32[3072]{0:T(1024)S(1)}) all-reduce(f32[2,768]{1,0:T(2,128)S(1)} %maximum_dynamic-update-slice_fusion, f32[6,768]{1,0:T(8,128)S(1)} %stack.44, f32[3072]{0:T(1024)S(1)} %dynamic_update_slice.24), channel_id=1, replica_groups=mesh['dp'=16,'tensor'=2] {'dp','tensor'}, use_global_device_ids=true, to_apply=%region_35.37 | all-reduce | flops 9216 | bytes 73728 | tf_op jit(solution)/shard_map/psum | solution.py:282
  1056.3 8.1 reshape.278
  1065.8 3.3 gather_fusion.3
  1069.1 3.5 fusion.148
  1072.7 27.9 %reduce-scatter.21.cloned.1.call-done = f32[48,1536]{1,0:T(8,128)} async-done(((f32[768,1536]{1,0:T(8,128)}), f32[48,1536]{1,0:T(8,128)}) %reduce-scatter.21.cloned.1.call-update) | async-done | bytes 294928 | tf_op jit(solution)/shard_map/reduce_scatter | solution.py:267
  1100.5 61.6 %reduce-scatter.19.cloned.1.call-done = f32[48,384]{1,0:T(8,128)} async-done(((f32[768,384]{1,0:T(8,128)}), f32[48,384]{1,0:T(8,128)}) %reduce-scatter.19.cloned.1.call-update) | async-done | bytes 73744 | tf_op jit(solution)/shard_map/reduce_scatter | solution.py:266
  1162.1 71.6 %reduce-scatter.17.cloned.1.call-done = f32[48,3,384]{2,0,1:T(8,128)} async-done(((f32[768,3,384]{2,0,1:T(8,128)}), f32[48,3,384]{2,0,1:T(8,128)}) %reduce-scatter.17.cloned.1.call-update) | async-done | bytes 221200 | tf_op jit(solution)/shard_map/reduce_scatter | solution.py:265
  (484 shorter events, 356.4 us)
Async XLA Ops:
  7.2 5.0 copy-start
  7.2 86.6 %all-gather.9.cloned.1.call-start = ((), (), s32[]{:S(2)}) async-start(), calls=%async_computation.13 | async-start | bytes 1880064 | tf_op jit(solution)/shard_map/all_gather | solution.py:145
  9.0 105.7 %all-gather.7.cloned.1.call-start = ((), (), s32[]{:S(2)}) async-start(), calls=%async_computation.12 | async-start | bytes 4718592 | tf_op jit(solution)/shard_map/all_gather | solution.py:157
  16.4 53.1 %copy-start.44 = (f32[2,384]{1,0:T(2,128)S(1)}, f32[2,384]{1,0:T(2,128)}, u32[]{:S(2)}) copy-start(f32[2,384]{1,0:T(2,128)} %param.30) | copy-start | bytes 9220
  16.4 53.3 %copy-start.31 = (f32[48,384]{1,0:T(8,128)S(1)}, f32[48,384]{1,0:T(8,128)}, u32[]{:S(2)}) copy-start(f32[48,384]{1,0:T(8,128)} %param.27) | copy-start | bytes 221188
  16.4 53.3 %copy-start.50 = (s32[16]{0:T(128)S(1)}, s32[16]{0:T(128)}, u32[]{:S(2)}) copy-start(s32[16]{0:T(128)} %param.24) | copy-start | bytes 196
  69.4 246.3 %reduce-scatter.9.cloned.1.call-start = ((), (), s32[]{:S(2)}) async-start(), calls=%async_computation.14 | async-start | bytes 4718592 | tf_op jit(solution)/shard_map/reduce_scatter | solution.py:171
  140.1 5.2 copy-start.11
  155.0 3.5 copy-start.5
  174.4 3.5 copy-start.5
  193.8 3.5 copy-start.5
  213.2 3.5 copy-start.5
  232.6 3.5 copy-start.5
  252.0 3.5 copy-start.5
  265.9 6.2 copy-start.2
  272.0 43.6 %copy-start.30 = (f32[768]{0:T(1024)S(1)}, f32[768]{0:T(1024)}, u32[]{:S(2)}) copy-start(f32[768]{0:T(1024)} %param.31) | copy-start | bytes 9220
  272.0 43.6 %copy-start.4 = (bf16[16,1,64,768]{3,2,1,0:T(8,128)(2,1)S(1)}, bf16[16,1,64,768]{3,2,1,0:T(8,128)(2,1)}, u32[]{:S(2)}) copy-start(bf16[16,1,64,768]{3,2,1,0:T(8,128)(2,1)} %all_to_all.42) | copy-start | bytes 4718596
  272.1 91.5 %all-gather.11.cloned.1.call-start = ((), (), s32[]{:S(2)}) async-start(), calls=%async_computation.15 | async-start | bytes 2506752 | tf_op jit(solution)/shard_map/all_gather | solution.py:147
  273.7 45.0 %copy-start.32 = (f32[768]{0:T(1024)S(1)}, f32[768]{0:T(1024)}, u32[]{:S(2)}) copy-start(f32[768]{0:T(1024)} %param.34) | copy-start | bytes 9220
  273.7 45.0 %copy-start.39 = (f32[768]{0:T(1024)S(1)}, f32[768]{0:T(1024)}, u32[]{:S(2)}) copy-start(f32[768]{0:T(1024)} %param.35) | copy-start | bytes 9220
  273.7 130.6 %all-gather.13.cloned.1.call-start = ((), (), s32[]{:S(2)}) async-start(), calls=%async_computation.16 | async-start | bytes 2506752 | tf_op jit(solution)/shard_map/all_gather | solution.py:148
  320.8 36.3 %collective-permute-start = (bf16[1024,768]{1,0:T(8,128)(2,1)}, bf16[1024,768]{1,0:T(8,128)(2,1)}, u32[]{:S(2)}, u32[]{:S(2)}) collective-permute-start(bf16[1024,768]{1,0:T(8,128)(2,1)} %fusion.144), channel_id=1, source_target_pairs={{0,1},{1,0},{2,3},{3,2},{4,5},{5,4},{6,7},{7,6},{8,9},{9,8},{10,11... | collective-permute-start | bytes 4718600 | tf_op jit(solution)/shard_map/ppermute | solution.py:14
  321.8 134.2 %reduce-scatter.11.cloned.1.call-start = ((), (), s32[]{:S(2)}) async-start(), calls=%async_computation.17 | async-start | bytes 4718592 | tf_op jit(solution)/shard_map/reduce_scatter | solution.py:185
  321.9 41.7 %copy-start.49 = (f32[1536]{0:T(1024)S(1)}, f32[1536]{0:T(1024)}, u32[]{:S(2)}) copy-start(f32[1536]{0:T(1024)} %param.32) | copy-start | bytes 18436
  413.3 41.2 %copy-start.33 = (f32[768]{0:T(1024)S(1)}, f32[768]{0:T(1024)}, u32[]{:S(2)}) copy-start(f32[768]{0:T(1024)} %param.36) | copy-start | bytes 9220
  413.4 42.6 %copy-start.42 = (f32[768]{0:T(1024)S(1)}, f32[768]{0:T(1024)}, u32[]{:S(2)}) copy-start(f32[768]{0:T(1024)} %param.33) | copy-start | bytes 9220
  413.4 97.4 %all-gather.15.cloned.1.call-start = ((), (), s32[]{:S(2)}) async-start(), calls=%async_computation.18 | async-start | bytes 4718592 | tf_op jit(solution)/shard_map/all_gather | solution.py:206
  465.5 110.4 %reduce-scatter.13.cloned.1.call-start = ((), (), s32[]{:S(2)}) async-start(), calls=%async_computation.19 | async-start | bytes 4718592 | tf_op jit(solution)/shard_map/reduce_scatter | solution.py:213
  510.8 15.1 %copy-start.48 = (bf16[768,1536]{1,0:T(8,128)(2,1)S(1)}, bf16[768,1536]{1,0:T(8,128)(2,1)}, u32[]{:S(2)}) copy-start(bf16[768,1536]{1,0:T(8,128)(2,1)} %all-gather.11.cloned.1.call-done) | copy-start | bytes 7077892
  532.3 98.6 %all-gather.17.cloned.1.call-start = ((), (), s32[]{:S(2)}) async-start(), calls=%async_computation.20 | async-start | bytes 4718592 | tf_op jit(solution)/shard_map/all_gather | solution.py:225
  575.9 4.6 copy-start.10
  575.9 4.6 copy-start.21
  584.5 46.4 %copy-start.27 = (bf16[768,384]{1,0:T(8,128)(2,1)S(1)}, bf16[768,384]{1,0:T(8,128)(2,1)}, u32[]{:S(2)}) copy-start(bf16[768,384]{1,0:T(8,128)(2,1)} %all_gather.27) | copy-start | bytes 1769476
  585.8 351.1 %reduce-scatter.15.cloned.1.call-start = ((), (), s32[]{:S(2)}) async-start(), calls=%async_computation.21 | async-start | bytes 4718592 | tf_op jit(solution)/shard_map/reduce_scatter | solution.py:256
  637.1 4.0 copy-start.3
  641.2 3.7 copy-start.6
  677.4 3.6 copy-start.6
  713.6 3.6 copy-start.6
  749.7 3.6 copy-start.6
  785.9 3.6 copy-start.6
  822.0 3.6 copy-start.6
  858.4 2.8 copy-start.16
  858.4 4.4 copy-start.14
  873.0 199.7 %reduce-scatter.23.cloned.1.call-start = ((), (), s32[]{:S(2)}) async-start(), calls=%async_computation.25 | async-start | bytes 5013504 | tf_op jit(solution)/shard_map/reduce_scatter | solution.py:268
  884.4 216.1 %reduce-scatter.21.cloned.1.call-start = ((), (), s32[]{:S(2)}) async-start(), calls=%async_computation.24 | async-start | bytes 5013504 | tf_op jit(solution)/shard_map/reduce_scatter | solution.py:267
  895.8 266.4 %reduce-scatter.19.cloned.1.call-start = ((), (), s32[]{:S(2)}) async-start(), calls=%async_computation.23 | async-start | bytes 1253376 | tf_op jit(solution)/shard_map/reduce_scatter | solution.py:266
  917.8 10.4 copy-start.24
  917.8 10.4 copy-start.25
  922.5 46.1 %all-to-all-start.1 = ((bf16[16,2,24576]{2,1,0:T(2,128)(2,1)}), bf16[16,2,24576]{2,1,0:T(2,128)(2,1)}, u32[]{:S(2)}, u32[]{:S(2)}) async-start(bf16[16,2,24576]{2,1,0:T(2,128)(2,1)} %reshape.275), calls=%async_computation.3 | async-start | bytes 3145728 | tf_op jit(solution)/shard_map/all_to_all | solution.py:286
  928.1 305.6 %reduce-scatter.17.cloned.1.call-start = ((), (), s32[]{:S(2)}) async-start(), calls=%async_computation.22 | async-start | bytes 3760128 | tf_op jit(solution)/shard_map/reduce_scatter | solution.py:265
  954.8 33.0 %copy-start.46 = (s32[16]{0:T(128)S(1)}, s32[16]{0:T(128)}, u32[]{:S(2)}) copy-start(s32[16]{0:T(128)} %get-tuple-element.277) | copy-start | bytes 196
  954.8 33.1 %copy-start.37 = (f32[768]{0:T(1024)S(1)}, f32[768]{0:T(1024)}, u32[]{:S(2)}) copy-start(f32[768]{0:T(1024)} %get-tuple-element.194) | copy-start | bytes 9220
  954.8 33.1 %copy-start.40 = (f32[768]{0:T(1024)S(1)}, f32[768]{0:T(1024)}, u32[]{:S(2)}) copy-start(f32[768]{0:T(1024)} %get-tuple-element.189) | copy-start | bytes 9220
  968.6 87.7 %all-to-all-start.3 = ((bf16[16,2,24576]{2,1,0:T(2,128)(2,1)}), bf16[16,2,24576]{2,1,0:T(2,128)(2,1)}, u32[]{:S(2)}, u32[]{:S(2)}) async-start(bf16[16,2,24576]{2,1,0:T(2,128)(2,1)} %reshape.277), calls=%async_computation.7 | async-start | bytes 3145728 | tf_op jit(solution)/shard_map/all_to_all | solution.py:289
  997.9 6.8 copy-start.41
  997.9 7.1 copy-start.36
  997.9 7.1 copy-start.35
  997.9 7.1 copy-start.34
  997.9 7.1 copy-start.38
  997.9 7.2 copy-start.17
  1001.4 4.0 copy-start.15
  1064.4 4.7 copy-start.45
  1065.8 3.3 copy-start.20
  1069.1 164.6 %copy-start.1 = (bf16[16,1,64,768]{3,2,1,0:T(8,128)(2,1)S(1)}, bf16[16,1,64,768]{3,2,1,0:T(8,128)(2,1)}, u32[]{:S(2)}) copy-start(bf16[16,1,64,768]{3,2,1,0:T(8,128)(2,1)} %param.23) | copy-start | bytes 4718596
  (25 other events, 45.2 us)
Sparse Core Ops, SparseCore 0:
  10.9 53.5 all-gather.8
  69.5 45.1 all-gather.6
  272.2 43.4 reduce-scatter.8
  318.4 42.1 all-gather.10
  363.2 41.0 all-gather.12
  413.5 42.1 reduce-scatter.10
  465.6 45.1 all-gather.14
  532.4 43.3 reduce-scatter.12
  586.0 44.9 all-gather.16
  873.1 43.3 reduce-scatter.14
  921.0 94.4 reduce-scatter.22
  1019.8 80.7 reduce-scatter.20
  1104.7 57.3 reduce-scatter.18
  1166.4 67.2 reduce-scatter.16
